TPU v7x, 128 devices: a whole 4x4x4 slice. The times are simulated.
128 devices in a mesh: layer: 8 (over z_lo, y), lat: 16 (over x, z_hi, core).
Axes of the slice: x: 4, y: 4, z: 4 (z_hi: 2, z_lo: 2; z = z_hi * 2 + z_lo), core: 2. Of those that a mesh axis runs over, the one named last changes fastest.
Arguments:
- activations: bfloat16 [8, 512, 2048], P(None, None, 'layer'), may hold values from -6 to 6
- targets: bfloat16 [8, 512, 2048], P(None, None, 'layer'), may hold values from -6 to 6
- encoder: bfloat16 [8, 2048, 8192], P(None, 'layer', 'lat'), may hold values from -0.125 to 0.125
- bias: float32 [8, 8192], P(None, 'lat'), may hold values from -3 to 3
- decoder: bfloat16 [36, 8192, 2048], P(None, 'lat', 'layer'), may hold values from -0.75 to 0.75
- active: int32 [8, 512, 64], replicated, may hold values from 0 to 8191, all different within a row
Outputs:
- grad_encoder: bfloat16 [8, 2048, 8192], P(None, 'layer', 'lat')
- grad_bias: float32 [8, 8192], P(None, 'lat')
- grad_decoder: bfloat16 [36, 8192, 2048], P(None, 'lat', 'layer')
Inputs may be any that keep to these rules, and one draw needn't show every extreme that they name: `active`: each row names 64 different latents.
All inputs are finite; a program needn't handle non-finite values.
Results may differ from a plain program's by a relative error of at most 0.0064.
Values may be sent and summed in bfloat16 or wider, within the bound.
No kernel may reach another device: no remote copies, remote signals or barrier semaphores. Data moves between devices by JAX's collectives and lax.ppermute only.
A program may use at most 128 MiB of HBM per device.

v0:
```python
import jax
import jax.numpy as jnp
from jax import lax
from jax.sharding import PartitionSpec as P

LAYERS = 8


def padded_to(lines, size):
    spare = -len(lines) % size
    return jnp.pad(lines, [(0, spare)] + [(0, 0)] * (lines.ndim - 1))


def sum_by_parts(x, axis):
    lines = x.reshape(-1, *x.shape[1:][-1:])
    own = lax.psum_scatter(
        padded_to(lines, lax.axis_size(axis)), axis, scatter_dimension=0, tiled=True
    )
    whole = lax.all_gather(own, axis).reshape(-1, *lines.shape[1:])
    return lax.slice_in_dim(whole, 0, len(lines)).reshape(x.shape)


def pair_index(source, target):
    return source * LAYERS - source * (source - 1) // 2 + (target - source)


def on_device(activations, targets, encoder, bias, decoder, active):
    lat_width = encoder.shape[2]
    first = lax.axis_index("lat") * lat_width
    columns = first + jnp.arange(lat_width, dtype=jnp.int32)
    masks = jnp.stack(
        [
            jnp.any(active[source][:, :, None] == columns[None, None, :], axis=1)
            for source in range(LAYERS)
        ]
    ).astype(jnp.float32)
    partial_value = jnp.einsum(
        "ltd,ldf->ltf", activations, encoder, preferred_element_type=jnp.float32
    )
    preact = lax.psum(partial_value, "layer") + bias[:, None, :]
    latent_act = (preact * masks).astype(jnp.bfloat16)
    rebuilt_list = []
    for target in range(LAYERS):
        summed = jnp.dot(
            latent_act[0], decoder[pair_index(0, target)], preferred_element_type=jnp.float32
        )
        for source in range(1, target + 1):
            summed = summed + jnp.dot(
                latent_act[source],
                decoder[pair_index(source, target)],
                preferred_element_type=jnp.float32,
            )
        rebuilt_list.append(summed)
    rebuilt = jnp.stack(rebuilt_list)
    complete = lax.psum(rebuilt, "lat")
    errors = (complete - targets.astype(jnp.float32)).astype(jnp.bfloat16)
    by_tokens = (((0,), (0,)), ((), ()))
    by_width = (((1,), (1,)), ((), ()))
    grad_pairs = []
    for source in range(LAYERS):
        for target in range(source, LAYERS):
            grad_pairs.append(
                lax.dot_general(
                    latent_act[source],
                    errors[target],
                    by_tokens,
                    preferred_element_type=jnp.float32,
                ).astype(jnp.bfloat16)
            )
    grad_decoder = jnp.stack(grad_pairs)
    grad_list = []
    for source in range(LAYERS):
        summed = lax.dot_general(
            errors[source],
            decoder[pair_index(source, source)],
            by_width,
            preferred_element_type=jnp.float32,
        )
        for target in range(source + 1, LAYERS):
            summed = summed + lax.dot_general(
                errors[target],
                decoder[pair_index(source, target)],
                by_width,
                preferred_element_type=jnp.float32,
            )
        grad_list.append(summed)
    grad_partial = jnp.stack(grad_list)
    grad_act = sum_by_parts(grad_partial, "layer")
    grad_pre = (grad_act * masks).astype(jnp.bfloat16)
    grad_encoder = jnp.einsum(
        "ltd,ltf->ldf", activations, grad_pre, preferred_element_type=jnp.float32
    ).astype(jnp.bfloat16)
    grad_bias = jnp.sum(grad_pre.astype(jnp.float32), axis=1)
    return (grad_encoder, grad_bias, grad_decoder)


def solution(mesh):
    placed = (
        P(None, None, "layer"),
        P(None, None, "layer"),
        P(None, "layer", "lat"),
        P(None, "lat"),
        P(None, "lat", "layer"),
        P(),
    )
    return jax.shard_map(
        on_device,
        mesh=mesh,
        in_specs=placed,
        out_specs=(P(None, "layer", "lat"), P(None, "lat"), P(None, "lat", "layer")),
        check_vma=False,
    )
```

profile of v0, /device:TPU:1, one launch (start us, length us, event | category | flops | bytes accessed | tf_op | source)
XLA Modules:
  0.0 620.0 jit_solution(13394112168313899540)
XLA Ops:
  8.8 6.2 %fusion.261 = f32[8,512,512]{2,1,0:T(8,128)} fusion(bf16[8,512,256]{2,1,0:T(8,128)(2,1)S(1)} %copy-done, bf16[8,256,512]{2,1,0:T(8,128)(2,1)} %param.8), kind=kOutput, calls=%fused_computation.401 | convolution fusion | flops 1073741824 | bytes 12582912 | tf_op jit(solution)/shard_map/ltd,ldf->ltf/dot_general | solution.py:37
  18.3 1.7 copy.21
  20.0 1.8 copy.22
  21.8 1.7 copy.23
  23.5 1.8 copy.24
  25.3 1.7 copy.25
  27.9 141.9 %compare_reduce_fusion = (pred[512,512]{1,0:T(8,128)(4,1)S(1)}, pred[512,512]{1,0:T(8,128)(4,1)}, pred[512,512]{1,0:T(8,128)(4,1)}, pred[512,512]{1,0:T(8,128)(4...) fusion(s32[512,64]{1,0:T(8,128)S(1)} %copy.26, ...), kind=kLoop, calls=%fused_computation | loop fusion | flops 266338304 | bytes 3147776 | tf_op jit(solution)/shard_map/reduce_or | solution.py:33
  173.1 1.7 bitcast_dynamic-update-slice_fusion.5
  180.3 22.3 %all-reduce.3.cloned.1.call-done = f32[8,512,512]{2,1,0:T(8,128)} async-done(((f32[8,512,512]{2,1,0:T(8,128)}), f32[8,512,512]{2,1,0:T(8,128)}) %all-reduce.3.cloned.1.call-update) | async-done | bytes 8388624 | tf_op jit(solution)/shard_map/psum | solution.py:40
  202.6 5.9 select_convert_fusion.1
  208.6 2.3 fusion.15
  232.1 150.0 %all-reduce.5.cloned.1.call-done = f32[8,512,256]{2,1,0:T(8,128)} async-done(((f32[8,512,256]{2,1,0:T(8,128)}), f32[8,512,256]{2,1,0:T(8,128)}) %all-reduce.5.cloned.1.call-update) | async-done | bytes 4194320 | tf_op jit(solution)/shard_map/psum | solution.py:55
  382.1 3.5 subtract_convert_fusion
  385.6 2.8 fusion.185
  406.0 3.4 copy-done.5
  409.7 94.0 %reduce-scatter.2.cloned.1.call-done = f32[512,512]{1,0:T(8,128)} async-done(((f32[4096,512]{1,0:T(8,128)}), f32[512,512]{1,0:T(8,128)}) %reduce-scatter.2.cloned.1.call-update) | async-done | bytes 1048592 | tf_op jit(solution)/shard_map/reduce_scatter | solution.py:16
  503.8 2.3 fusion.31
  506.1 2.2 fusion.33
  508.2 2.2 fusion.35
  510.4 2.0 fusion.37
  546.0 49.8 %all-gather.3.cloned.1.call-done = f32[4096,512]{1,0:T(8,128)} async-done(((f32[512,512]{1,0:T(8,128)}), f32[4096,512]{1,0:T(8,128)}) %all-gather.3.cloned.1.call-update) | async-done | bytes 8388624 | tf_op jit(solution)/shard_map/all_gather | solution.py:19
  595.8 7.5 %convert_bitcast_fusion = bf16[8,256,512]{1,2,0:T(8,128)(2,1)} fusion(bf16[8,512,256]{2,1,0:T(8,128)(2,1)S(1)} %copy-done, pred[8,512,512]{2,1,0:T(8,128)(4,1)} %bitcast_dynamic-update-slice_fusion, f32[8,512,512]{2,1,0:T(8,128)} %bitcast.608), kind=kOutput, calls=%fused_computation.12 | convolution fusion | flops 1076887552 | bytes 14680064 | tf_op jit(solution)/shard_map/ltd,ltf->ldf/dot_general | solution.py:90
  603.3 3.9 copy.28
  607.2 6.0 convert_reduce_fusion
  (151 shorter events, 86.7 us)
Async XLA Ops:
  7.2 1.6 copy-start
  7.2 195.4 %all-reduce.3.cloned.1.call-start = ((), (), s32[]{:S(2)}) async-start(), calls=%async_computation.1 | async-start | bytes 16777216 | tf_op jit(solution)/shard_map/psum | solution.py:40
  15.0 1.2 copy-start.6
  15.0 367.0 %all-reduce.5.cloned.1.call-start = ((), (), s32[]{:S(2)}) async-start(), calls=%async_computation.2 | async-start | bytes 8388608 | tf_op jit(solution)/shard_map/psum | solution.py:55
  27.9 174.7 %copy-start.7 = (f32[8,512]{1,0:T(8,128)S(1)}, f32[8,512]{1,0:T(8,128)}, u32[]{:S(2)}) copy-start(f32[8,512]{1,0:T(8,128)} %param.9) | copy-start | bytes 49156
  202.6 14.6 %slice-start = ((s8[9437184]{0:T(1024)(128)(4,1)}), s8[4194304]{0:T(1024)(128)(4,1)S(1)}, s32[]{:S(2)}) async-start(s8[9437184]{0:T(1024)(128)(4,1)} %bitcast.604), calls=%async_computation.5 | async-start | bytes 8388608
  202.6 14.6 %slice-start.1 = ((s8[9437184]{0:T(1024)(128)(4,1)}), s8[4194304]{0:T(1024)(128)(4,1)S(1)}, s32[]{:S(2)}) async-start(s8[9437184]{0:T(1024)(128)(4,1)} %bitcast.604), calls=%async_computation.6 | async-start | bytes 8388608
  208.5 22.2 %copy-start.1 = (bf16[8,512,512]{2,1,0:T(8,128)(2,1)}, bf16[8,512,512]{2,1,0:T(8,128)(2,1)S(1)}, u32[]{:S(2)}) copy-start(bf16[8,512,512]{2,1,0:T(8,128)(2,1)S(1)} %select_convert_fusion.1) | copy-start | bytes 12582916
  208.6 8.6 %slice-start.2 = ((s8[9437184]{0:T(1024)(128)(4,1)}), s8[1048576]{0:T(1024)(128)(4,1)S(1)}, s32[]{:S(2)}) async-start(s8[9437184]{0:T(1024)(128)(4,1)} %bitcast.604), calls=%async_computation.7 | async-start | bytes 2097152
  231.8 271.9 %reduce-scatter.2.cloned.1.call-start = ((), (), s32[]{:S(2)}) async-start(), calls=%async_computation.3 | async-start | bytes 9437184 | tf_op jit(solution)/shard_map/reduce_scatter | solution.py:16
  382.1 14.1 %slice-start.3 = ((s8[9437184]{0:T(1024)(128)(4,1)}), s8[4194304]{0:T(1024)(128)(4,1)S(1)}, s32[]{:S(2)}) async-start(s8[9437184]{0:T(1024)(128)(4,1)} %bitcast.606), calls=%async_computation.8 | async-start | bytes 8388608
  382.1 14.2 %slice-start.4 = ((s8[9437184]{0:T(1024)(128)(4,1)}), s8[4194304]{0:T(1024)(128)(4,1)S(1)}, s32[]{:S(2)}) async-start(s8[9437184]{0:T(1024)(128)(4,1)} %bitcast.606), calls=%async_computation.9 | async-start | bytes 8388608
  385.6 20.1 %copy-start.3 = (bf16[8,512,256]{2,1,0:T(8,128)(2,1)}, bf16[8,512,256]{2,1,0:T(8,128)(2,1)S(1)}, u32[]{:S(2)}) copy-start(bf16[8,512,256]{2,1,0:T(8,128)(2,1)S(1)} %subtract_convert_fusion) | copy-start | bytes 6291460
  389.7 6.5 %slice-start.5 = ((s8[9437184]{0:T(1024)(128)(4,1)}), s8[1048576]{0:T(1024)(128)(4,1)S(1)}, s32[]{:S(2)}) async-start(s8[9437184]{0:T(1024)(128)(4,1)} %bitcast.606), calls=%async_computation.10 | async-start | bytes 2097152
  406.0 3.4 copy-start.5
  409.4 186.4 %all-gather.3.cloned.1.call-start = ((), (), s32[]{:S(2)}) async-start(), calls=%async_computation.4 | async-start | bytes 9437184 | tf_op jit(solution)/shard_map/all_gather | solution.py:19
  503.7 6.7 %copy-start.2 = (bf16[8,512,512]{2,1,0:T(8,128)(2,1)S(1)}, bf16[8,512,512]{2,1,0:T(8,128)(2,1)}, u32[]{:S(2)}) copy-start(bf16[8,512,512]{2,1,0:T(8,128)(2,1)} %copy-done.1) | copy-start | bytes 12582916
  503.7 8.6 %copy-start.4 = (bf16[8,512,256]{2,1,0:T(8,128)(2,1)S(1)}, bf16[8,512,256]{2,1,0:T(8,128)(2,1)}, u32[]{:S(2)}) copy-start(bf16[8,512,256]{2,1,0:T(8,128)(2,1)} %copy-done.3) | copy-start | bytes 6291460
Sparse Core Ops, SparseCore 0:
  15.2 187.3 all-reduce.2
  232.0 150.0 all-reduce.4
  409.6 94.1 reduce-scatter.1
  505.2 90.5 all-gather.2
where the time goes:
time: 626 us; the launch traced here: 620 us
  waiting for transfers between devices  316 us (50%)
  other arithmetic  157 us (25%)
  matrix products  99 us (16%)
  local copies, waits for them, and re-layouts  32.2 us (5%)
  between operations  14.7 us (2%)
    psum x1, waiting for transfers between devices, on_device(): complete = lax.psum(rebuilt, 'lat')  150 us
    reduce_or x1, other arithmetic, on_device(): jnp.any(active[source][:, :, None] == columns[None, None, :], axis=1)  142 us
    reduce_scatter x1, waiting for transfers between devices, sum_by_parts(): lax.psum_scatter(padded_to(lines, lax.axis_size(axis)), axis, scatter_dim...  94 us
    all_gather x1, waiting for transfers between devices, sum_by_parts(): whole = lax.all_gather(own, axis).reshape(-1, *lines.shape[1:])  49.8 us
    dot_general x36, matrix products, on_device(): lax.dot_general(latent_act[source], errors[target], by_tokens, preferred_...  42.3 us
    psum x1, waiting for transfers between devices, on_device(): preact = lax.psum(partial_value, 'layer') + bias[:, None, :]  22.3 us
    unnamed x36, local copies, waits for them, and re-layouts  19.8 us
    dot_general x28, matrix products, on_device(): jnp.dot(latent_act[source], decoder[pair_index(source, target)], preferre...  13.8 us
  transfers between devices with their start and end apart: 4, of which 4 were waited for; matrix products, arithmetic and copies ran while one was open for 33% of the time, Pallas kernels for 0%

commit v1 on v0

--- a/solution.py
+++ b/solution.py
@@ -37,7 +37,7 @@
     partial_value = jnp.einsum(
         "ltd,ldf->ltf", activations, encoder, preferred_element_type=jnp.float32
     )
-    preact = lax.psum(partial_value, "layer") + bias[:, None, :]
+    preact = jnp.sum(lax.all_gather(partial_value, "layer"), axis=0) + bias[:, None, :]
     latent_act = (preact * masks).astype(jnp.bfloat16)
     rebuilt_list = []
     for target in range(LAYERS):

time: 626 us -> 1110 us (1.77)
  waiting for transfers between devices: 316 us -> 776 us
  other arithmetic: 157 us -> 182 us
    all_gather x0 -> x1, waiting for transfers between devices: none -> 482 us  [on_device(): lax.all_gather(partial_value, 'layer')]
    reduce_sum x0 -> x1, other arithmetic: none -> 25.4 us  [on_device(): jnp.sum(lax.all_gather(partial_value, 'layer'), axis=0) + bias[:, None, :]]
    psum x1 -> x0, waiting for transfers between devices: 22.3 us -> none  [on_device(): preact = lax.psum(partial_value, 'layer') + bias[:, None, :]]
  transfers between devices with their start and end apart: 4 -> 4, of which waited for: 4 -> 4; matrix products, arithmetic and copies ran while one was open for 33% -> 19% of each run, Pallas kernels for 0% -> 0%
where the time goes in v1:
time: 1110 us; the launch traced here: 1100 us
  waiting for transfers between devices  776 us (70%)
  other arithmetic  182 us (16%)
  matrix products  99.2 us (9%)
  local copies, waits for them, and re-layouts  31.5 us (3%)
  between operations  14.7 us (1%)
    all_gather x1, waiting for transfers between devices, on_device(): lax.all_gather(partial_value, 'layer')  482 us
    psum x1, waiting for transfers between devices, on_device(): complete = lax.psum(rebuilt, 'lat')  150 us
    reduce_or x1, other arithmetic, on_device(): jnp.any(active[source][:, :, None] == columns[None, None, :], axis=1)  141 us
    reduce_scatter x1, waiting for transfers between devices, sum_by_parts(): lax.psum_scatter(padded_to(lines, lax.axis_size(axis)), axis, scatter_dim...  93.9 us
    all_gather x1, waiting for transfers between devices, sum_by_parts(): whole = lax.all_gather(own, axis).reshape(-1, *lines.shape[1:])  49.8 us
    dot_general x36, matrix products, on_device(): lax.dot_general(latent_act[source], errors[target], by_tokens, preferred_...  42.2 us
    reduce_sum x1, other arithmetic, on_device(): jnp.sum(lax.all_gather(partial_value, 'layer'), axis=0) + bias[:, None, :]  25.4 us
  transfers between devices with their start and end apart: 4, of which 4 were waited for; matrix products, arithmetic and copies ran while one was open for 19% of the time, Pallas kernels for 0%

profile of v1, /device:TPU:1, one launch (start us, length us, event | category | flops | bytes accessed | tf_op | source)
XLA Modules:
  0.0 1103.4 jit_solution(11333060449312312756)
XLA Ops:
  8.8 6.2 fusion.261
  18.4 1.7 copy.41
  20.1 1.7 copy.40
  21.8 1.7 copy.39
  23.6 1.7 copy.45
  26.2 141.1 %compare_reduce_fusion = (pred[512,512]{1,0:T(8,128)(4,1)S(1)}, pred[512,512]{1,0:T(8,128)(4,1)}, pred[512,512]{1,0:T(8,128)(4,1)}, pred[512,512]{1,0:T(8,128)(4...) fusion(s32[512,64]{1,0:T(8,128)} %copy.45, ...), kind=kLoop, calls=%fused_computation | loop fusion | flops 266338304 | bytes 3147776 | tf_op jit(solution)/shard_map/reduce_or | solution.py:33
  172.3 1.7 bitcast_dynamic-update-slice_fusion.4
  175.7 1.7 bitcast_dynamic-update-slice_fusion.2
  178.8 481.9 %all-gather.5.cloned.1.call-done = f32[64,512,512]{2,1,0:T(8,128)} async-done(((f32[8,512,512]{2,1,0:T(8,128)}), f32[64,512,512]{2,1,0:T(8,128)}) %all-gather.5.cloned.1.call-update) | async-done | bytes 67108880 | tf_op jit(solution)/shard_map/all_gather | solution.py:40
  660.7 25.4 %reduce_sum.18 = f32[8,512,512]{2,1,0:T(8,128)} reduce(f32[8,8,512,512]{3,2,1,0:T(8,128)} %bitcast.16, f32[]{:T(128)} %constant.12.clone.1), dimensions={0}, to_apply=%region_8.0 | reduce | flops 14680064 | bytes 75497472 | tf_op jit(solution)/shard_map/reduce_sum | solution.py:40
  686.1 5.9 select_convert_fusion.1
  715.7 149.9 %all-reduce.2.cloned.1.call-done = f32[8,512,256]{2,1,0:T(8,128)} async-done(((f32[8,512,256]{2,1,0:T(8,128)}), f32[8,512,256]{2,1,0:T(8,128)}) %all-reduce.2.cloned.1.call-update) | async-done | bytes 4194320 | tf_op jit(solution)/shard_map/psum | solution.py:55
  865.6 3.5 subtract_convert_fusion
  869.1 2.8 fusion.119
  889.6 3.4 copy-done.5
  893.2 93.9 %reduce-scatter.2.cloned.1.call-done = f32[512,512]{1,0:T(8,128)} async-done(((f32[4096,512]{1,0:T(8,128)}), f32[512,512]{1,0:T(8,128)}) %reduce-scatter.2.cloned.1.call-update) | async-done | bytes 1048592 | tf_op jit(solution)/shard_map/reduce_scatter | solution.py:16
  987.2 2.3 fusion.31
  989.5 2.2 fusion.33
  991.7 2.2 fusion.35
  993.9 2.0 fusion.37
  1029.5 49.8 %all-gather.7.cloned.1.call-done = f32[4096,512]{1,0:T(8,128)} async-done(((f32[512,512]{1,0:T(8,128)}), f32[4096,512]{1,0:T(8,128)}) %all-gather.7.cloned.1.call-update) | async-done | bytes 8388624 | tf_op jit(solution)/shard_map/all_gather | solution.py:19
  1079.3 7.5 convert_bitcast_fusion
  1086.7 3.9 copy.47
  1090.6 6.0 convert_reduce_fusion
  (152 shorter events, 88.6 us)
Async XLA Ops:
  7.2 1.6 copy-start
  7.2 653.5 %all-gather.5.cloned.1.call-start = ((), (), s32[]{:S(2)}) async-start(), calls=%async_computation.3 | async-start | bytes 75497472 | tf_op jit(solution)/shard_map/all_gather | solution.py:40
  15.0 1.2 copy-start.6
  15.0 850.6 %all-reduce.2.cloned.1.call-start = ((), (), s32[]{:S(2)}) async-start(), calls=%async_computation.1 | async-start | bytes 8388608 | tf_op jit(solution)/shard_map/psum | solution.py:55
  660.7 25.4 %copy-start.7 = (f32[8,512]{1,0:T(8,128)S(1)}, f32[8,512]{1,0:T(8,128)}, u32[]{:S(2)}) copy-start(f32[8,512]{1,0:T(8,128)} %param.9) | copy-start | bytes 49156
  686.1 14.0 %slice-start = ((s8[9437184]{0:T(1024)(128)(4,1)}), s8[4194304]{0:T(1024)(128)(4,1)S(1)}, s32[]{:S(2)}) async-start(s8[9437184]{0:T(1024)(128)(4,1)} %bitcast.605), calls=%async_computation.5 | async-start | bytes 8388608
  686.1 14.0 %slice-start.1 = ((s8[9437184]{0:T(1024)(128)(4,1)}), s8[4194304]{0:T(1024)(128)(4,1)S(1)}, s32[]{:S(2)}) async-start(s8[9437184]{0:T(1024)(128)(4,1)} %bitcast.605), calls=%async_computation.6 | async-start | bytes 8388608
  692.0 22.4 %copy-start.1 = (bf16[8,512,512]{2,1,0:T(8,128)(2,1)}, bf16[8,512,512]{2,1,0:T(8,128)(2,1)S(1)}, u32[]{:S(2)}) copy-start(bf16[8,512,512]{2,1,0:T(8,128)(2,1)S(1)} %select_convert_fusion.1) | copy-start | bytes 12582916
  692.0 8.0 slice-start.2
  715.5 271.7 %reduce-scatter.2.cloned.1.call-start = ((), (), s32[]{:S(2)}) async-start(), calls=%async_computation.2 | async-start | bytes 9437184 | tf_op jit(solution)/shard_map/reduce_scatter | solution.py:16
  865.6 14.1 %slice-start.3 = ((s8[9437184]{0:T(1024)(128)(4,1)}), s8[4194304]{0:T(1024)(128)(4,1)S(1)}, s32[]{:S(2)}) async-start(s8[9437184]{0:T(1024)(128)(4,1)} %bitcast.607), calls=%async_computation.8 | async-start | bytes 8388608
  865.6 14.2 %slice-start.4 = ((s8[9437184]{0:T(1024)(128)(4,1)}), s8[4194304]{0:T(1024)(128)(4,1)S(1)}, s32[]{:S(2)}) async-start(s8[9437184]{0:T(1024)(128)(4,1)} %bitcast.607), calls=%async_computation.9 | async-start | bytes 8388608
  869.1 20.1 %copy-start.3 = (bf16[8,512,256]{2,1,0:T(8,128)(2,1)}, bf16[8,512,256]{2,1,0:T(8,128)(2,1)S(1)}, u32[]{:S(2)}) copy-start(bf16[8,512,256]{2,1,0:T(8,128)(2,1)S(1)} %subtract_convert_fusion) | copy-start | bytes 6291460
  873.2 6.5 slice-start.5
  889.6 3.4 copy-start.5
  893.0 186.3 %all-gather.7.cloned.1.call-start = ((), (), s32[]{:S(2)}) async-start(), calls=%async_computation.4 | async-start | bytes 9437184 | tf_op jit(solution)/shard_map/all_gather | solution.py:19
  987.2 6.7 copy-start.2
  987.2 8.6 copy-start.4
Sparse Core Ops, SparseCore 0:
  15.2 645.4 all-gather.4
  715.6 149.9 all-reduce.1
  893.1 94.0 reduce-scatter.1
  988.7 90.5 all-gather.6
